TPU v7x, 32 devices: a whole 2x2x4 slice. The times are simulated.
32 devices in a mesh: real: 2 (over x), row: 16 (over z, y, core).
Axes of the slice: x: 2, y: 2, z: 4, core: 2. Of those that a mesh axis runs over, the one named last changes fastest.
Arguments:
- site_tensor: float32 [32, 2, 256, 256], P(('real', 'row')), parts along dimension 0, may hold values from -20 to 20
- left_env: float32 [32, 14, 256, 256], P(('real', 'row')), parts along dimension 0, may hold values from -10 to 10
- right_env: float32 [32, 14, 256, 256], P(('real', 'row')), parts along dimension 0, may hold values from -10 to 10
- sector_size: int32 [32], P('real'), parts along dimension 0, may hold values from 64 to 256
Outputs:
- left_out: float32 [32, 2, 256, 256], P(('real', 'row')), parts along dimension 0
- bond_out: float32 [32, 256, 256], P(('real', 'row')), parts along dimension 0
There are 2 independent parts, one for each index of `real`. A program takes and returns all parts, laid end to end along the dimension named above; each array names one. Nothing has to cross between parts.
All inputs are finite; a program needn't handle non-finite values.
Results may differ from a plain program's by a relative error of at most 0.00005.
Values sent between devices are 32-bit elements; how exact they have to be, the bound alone decides.
A program may use at most 64 MiB of HBM per device.

v0:
```python
import functools

import jax
import jax.numpy as jnp
from jax import lax
from jax.experimental import pallas as pl
from jax.experimental.pallas import tpu as pltpu
from jax.sharding import PartitionSpec as P

W_DN = 4
W_UP = 4
PANEL = 16
TAU = 0.15
highest = lax.Precision.HIGHEST
f32 = jnp.float32
bf16 = jnp.bfloat16
MESH = pl.DeviceIdType.MESH


def dot(a, b):
    return jnp.dot(a, b, preferred_element_type=f32)


def split_2(value):
    high = value.astype(bf16)
    return high, (value - high.astype(f32)).astype(bf16)


def split_3(value):
    high = value.astype(bf16)
    rest = value - high.astype(f32)
    middle = rest.astype(bf16)
    return high, middle, (rest - middle.astype(f32)).astype(bf16)


def store_split(pair_ref, index, value):
    high, low = split_2(value)
    pair_ref[0, index] = high
    pair_ref[1, index] = low


def tile_sum(value):
    rows, columns = value.shape
    summed = jnp.sum(value.reshape(rows // 8, 8, columns), axis=0)
    total = summed[:, :128]
    for start in range(128, columns, 128):
        total = total + summed[:, start : start + 128]
    return total


def full_sum(tile):
    return jnp.sum(jnp.sum(tile, axis=0, keepdims=True), axis=1, keepdims=True)


def panel_step(p, lo, hi, states, aug_ref, out_ref):
    base = pl.multiple_of(p * PANEL, PANEL)
    row_id = lax.broadcasted_iota(jnp.int32, (PANEL, 128), 0)
    offset = lax.rem(p * PANEL, 128)
    diag = aug_ref[pl.ds(base, PANEL), lo : lo + 128]
    diag = pltpu.roll(diag, lax.rem(128 - offset, 128), 1)
    columns = [jnp.broadcast_to(diag[:, r : r + 1], (PANEL, 128)) for r in range(PANEL)]
    tiles = [aug_ref[pl.ds(base, PANEL), t : t + 128] for t in range(lo, hi, 128)]
    scale = jnp.zeros((PANEL, 128), f32)
    for r in range(PANEL):
        inverse = lax.rsqrt(columns[r][r : r + 1, :])
        scale = jnp.where(row_id == r, inverse, scale)
        multiplier = columns[r] * inverse
        below = jnp.where(row_id > r, multiplier, 0.0)
        for s in range(r + 1, PANEL):
            columns[s] = columns[s] - below * multiplier[s : s + 1, :]
        if r < PANEL - 1:
            tiles = [tile - below * (tile[r : r + 1, :] * inverse) for tile in tiles]
    tiles = [tile * scale for tile in tiles]
    for t, tile in zip(range(lo, hi, 128), tiles):
        out_ref[pl.ds(base, PANEL), t : t + 128] = tile
    panel = jnp.concatenate(tiles, 1)
    q1, q2, q3 = split_3(panel)
    p1, p2, p3 = (q[:, : states - lo] for q in (q1, q2, q3))
    left = jnp.concatenate([p1, p1, p2, p2, p1, p3], 0)
    right = jnp.concatenate([q1, q2, q1, q2, q3, q1], 0)
    update = lax.dot_general(left, right, (((0,), (0,)), ((), ())), preferred_element_type=f32)
    aug_ref[lo:states, lo:hi] -= update


def kernel(
    size_ref, site_hbm, left_hbm, right_hbm,
    left_out, bond_out,
    site, low, left_f, right_f, left_s, right_s, aug, fac, packed, bond, applied, acc, field_in, field_s,
    red_in, red_own, local_sem, send_sem, recv_sem, red_send, red_recv,
):
    count = lax.axis_size("row")
    me = lax.axis_index("row")
    states = site.shape[-1]
    channels = left_f.shape[0]
    moved = W_DN + W_UP
    not_first, not_last = me > 0, me < count - 1

    loads = [
        pltpu.make_async_copy(site_hbm.at[0], site, local_sem.at[0]),
        pltpu.make_async_copy(left_hbm.at[0], left_f, local_sem.at[1]),
        pltpu.make_async_copy(right_hbm.at[0, moved:], right_f.at[moved:], local_sem.at[2]),
    ]
    for load in loads:
        load.start()

    barrier = pltpu.get_barrier_semaphore()
    for step in range(1, count):
        peer = lax.rem(me + step, count)
        pl.semaphore_signal(barrier, inc=1, device_id={"row": peer}, device_id_type=MESH)
    pl.semaphore_wait(barrier, count - 1)

    def remote(source, target, slot, peer):
        return pltpu.make_async_remote_copy(
            src_ref=source, dst_ref=target, send_sem=send_sem.at[slot], recv_sem=recv_sem.at[slot],
            device_id={"row": peer}, device_id_type=MESH,
        )

    to_right, to_left = jnp.minimum(me + 1, count - 1), jnp.maximum(me - 1, 0)
    half = states // 2
    send_site = remote(site_hbm.at[0, 1], low, 0, to_right)
    send_down = [remote(right_hbm.at[0, a], right_f.at[a], 1 + a, to_right) for a in range(W_DN)]
    send_up = [remote(right_hbm.at[0, a], right_f.at[a], 1 + a, to_left) for a in range(W_DN, moved)]
    send_bond_right = [
        remote(packed.at[:half], field_in.at[0, 0, :half], moved + 1, to_right),
        remote(packed.at[half:, half:], field_in.at[0, 0, half:, half:], moved + 2, to_right),
    ]
    send_bond_left = remote(packed, field_in.at[0, 1], moved + 3, to_left)
    send_applied_right = remote(applied, field_in.at[1, 0], moved + 4, to_right)
    send_applied_left = remote(applied, field_in.at[1, 1], moved + 5, to_left)
    rightward = [send_site] + send_down + send_bond_right + [send_applied_right]
    leftward = send_up + [send_bond_left, send_applied_left]
    early_down, early_up = W_DN // 2, W_UP // 2

    @pl.when(not_last)
    def _():
        send_site.start()

    @pl.when(me == 0)
    def _():
        low[...] = jnp.zeros_like(low)
        right_f[:W_DN] = jnp.zeros((W_DN, states, states), f32)
        field_in[:, 0] = jnp.zeros((2, states, states), f32)

    @pl.when(me == count - 1)
    def _():
        right_f[W_DN:moved] = jnp.zeros((W_UP, states, states), f32)
        field_in[:, 1] = jnp.zeros((2, states, states), f32)

    size = size_ref[me]
    size_before = size_ref[to_left]
    size_after = size_ref[to_right]
    row = lax.broadcasted_iota(jnp.int32, (states, states), 0)
    column = lax.broadcasted_iota(jnp.int32, (states, states), 1)
    live_pair = (row < size) & (column < size)
    gram_dims = (((0,), (0,)), ((), ()))
    loads[0].wait()
    upper = jnp.where(live_pair, site[0], 0.0)
    site[0] = upper
    gram = lax.dot_general(upper, upper, gram_dims, precision=highest, preferred_element_type=f32)
    gram = gram + jnp.where((row == column) & (row >= size), 1.0, 0.0)
    aug[:, states:] = jnp.where(row == column, 1.0, 0.0).astype(f32)

    @pl.when(not_last)
    def _():
        send_site.wait_send()
        for one in send_down[:early_down]:
            one.start()

    @pl.when(not_first)
    def _():
        for one in send_up[:early_up]:
            one.start()
        send_site.wait_recv()

    lower = jnp.where((row < size_before) & (column < size), low[...], 0.0)
    aug[:, :states] = gram + lax.dot_general(lower, lower, gram_dims, precision=highest, preferred_element_type=f32)
    fac[...] = jnp.zeros_like(fac)
    loads[1].wait()
    loads[2].wait()

    halves = half // PANEL

    def first_half(p, carry):
        panel_step(p, 0, states + half, states, aug, fac)
        store_split(left_s, p, left_f[p])
        return carry

    def second_half(p, carry):
        panel_step(p, half, 2 * states, states, aug, fac)
        other = jnp.minimum(p, channels - 1)
        store_split(left_s, other, left_f[other])
        mine = jnp.minimum(p - halves + moved, channels - 1)
        store_split(right_s, mine, right_f[mine])
        return carry

    lax.fori_loop(0, halves, first_half, 0)
    lax.fori_loop(halves, 2 * halves, second_half, 0)

    packed[...] = jnp.where(column >= row, fac[:, :states], fac[:, states:])

    @pl.when(not_last)
    def _():
        for one in send_bond_right + send_down[early_down:]:
            one.start()

    @pl.when(not_first)
    def _():
        for one in [send_bond_left] + send_up[early_up:]:
            one.start()

    bond[...] = jnp.where(live_pair & (column >= row), fac[:, :states], 0.0)
    inverse = jnp.where(column <= row, fac[:, states:], 0.0)
    turned = (((1,), (1,)), ((), ()))
    left_out[0] = lax.dot_general(site[0], inverse, turned, precision=highest, preferred_element_type=f32)

    def put_field(which, value):
        field_s[which, 0], field_s[which, 1] = split_2(value)

    def add_terms(total, which, a):
        high, low_part = field_s[which, 0], field_s[which, 1]
        r_high, r_low = right_s[0, a], right_s[1, a]
        l_high, l_low = left_s[0, a], left_s[1, a]
        middle = dot(high, r_high) + dot(high, r_low) + dot(low_part, r_high)
        m_high, m_low = split_2(middle)
        return total + dot(l_high, m_high) + dot(l_high, m_low) + dot(l_low, m_high)

    def add_range(which, start, stop):
        group = 2 if (stop - start) % 2 == 0 else 1

        def some(g, carry):
            total = acc[...]
            for k in range(group):
                total = add_terms(total, which, start + g * group + k)
            acc[...] = total
            return carry

        lax.fori_loop(0, (stop - start) // group, some, 0)

    def take_moved(down, up):
        @pl.when(not_first)
        def _():
            for a in down:
                send_down[a].wait_recv()

        @pl.when(not_last)
        def _():
            for a in up:
                send_up[a - W_DN].wait_recv()

        for a in (*down, *up):
            store_split(right_s, a, right_f[a])

    acc[...] = jnp.zeros_like(acc)
    put_field(0, bond[...])
    add_range(0, moved, channels)
    take_moved(range(early_down), range(W_DN, W_DN + early_up))

    @pl.when(not_first)
    def _():
        for one in send_bond_right:
            one.wait_recv()

    put_field(1, jnp.where((column >= row) & (row < size_before) & (column < size_before), field_in[0, 0], 0.0))
    add_range(1, 0, early_down)

    @pl.when(not_last)
    def _():
        send_bond_left.wait_recv()

    near = field_in[0, 1]
    put_field(2, jnp.where((column >= row) & (row < size_after) & (column < size_after), near, 0.0))
    add_range(2, W_DN, W_DN + early_up)
    near_inverse = jnp.where(column < row, near, jnp.where(column == row, 1.0 / near, 0.0))
    outer = jnp.where((row < size) & (column < size_after), site[1], 0.0)
    outer = lax.dot_general(outer, near_inverse, turned, precision=highest, preferred_element_type=f32)
    left_out[1] = jnp.where(not_last, outer, 0.0)
    for k in range(max(W_DN - early_down, W_UP - early_up)):
        down = [early_down + k] if early_down + k < W_DN else []
        up = [W_DN + early_up + k] if early_up + k < W_UP else []
        take_moved(down, up)
        total = acc[...]
        for which, group in ((1, down), (2, up)):
            for a in group:
                total = add_terms(total, which, a)
        acc[...] = total

    def reductions(t):
        for step in range(1, count):
            peer = lax.rem(me + step, count)
            yield pltpu.make_async_remote_copy(
                src_ref=red_own.at[t], dst_ref=red_in.at[t, step],
                send_sem=red_send.at[t, step], recv_sem=red_recv.at[t, step],
                device_id={"row": peer}, device_id_type=MESH,
            )

    applied[...] = jnp.where(live_pair, acc[...], 0.0)

    @pl.when(not_last)
    def _():
        send_applied_right.start()

    @pl.when(not_first)
    def _():
        send_applied_left.start()

    red_own[0, :8] = tile_sum(bond[...] * bond[...])
    red_own[0, 8:] = tile_sum(bond[...] * applied[...])
    first_sums = list(reductions(0))
    for one in first_sums:
        one.start()

    acc[...] = jnp.zeros_like(acc)
    put_field(0, applied[...])
    add_range(0, moved, channels)

    @pl.when(not_first)
    def _():
        send_applied_right.wait_recv()

    put_field(1, field_in[1, 0])
    add_range(1, 0, W_DN)

    @pl.when(not_last)
    def _():
        send_applied_left.wait_recv()

    put_field(2, field_in[1, 1])
    add_range(2, W_DN, moved)

    def collect(t, copies):
        total = red_own[t]
        for step, one in enumerate(copies, 1):
            one.wait_recv()
            total = total + red_in[t, step]
        return total

    total = collect(0, first_sums)
    start_norm = full_sum(total[:8])
    energy = full_sum(total[8:]) / start_norm
    shifted = applied[...] - energy * bond[...]
    second = jnp.where(live_pair, acc[...], 0.0) - energy * applied[...] - energy * shifted
    acc[...] = bond[...] + TAU * shifted + (0.5 * TAU * TAU) * second
    red_own[1, :8] = tile_sum(acc[...] * acc[...])
    red_own[1, 8:] = jnp.zeros((8, 128), f32)
    second_sums = list(reductions(1))
    for one in second_sums:
        one.start()

    @pl.when(not_last)
    def _():
        for one in rightward[1:]:
            one.wait_send()

    @pl.when(not_first)
    def _():
        for one in leftward:
            one.wait_send()

    final_norm = full_sum(collect(1, second_sums)[:8])
    bond_out[...] = acc[...] * jnp.sqrt(start_norm / final_norm)
    for one in first_sums + second_sums:
        one.wait_send()


def write_out(left, bond, left_hbm, bond_hbm, sem):
    stores = [
        pltpu.make_async_copy(left, left_hbm.at[0], sem.at[0]),
        pltpu.make_async_copy(bond, bond_hbm.at[0], sem.at[1]),
    ]
    for store in stores:
        store.start()
    for store in stores:
        store.wait()


def on_device(site_tensor, left_env, right_env, sector_size):
    states = site_tensor.shape[-1]
    channels = left_env.shape[1]
    count = lax.axis_size("row")
    block = (states, states)
    anywhere = pl.BlockSpec(memory_space=pl.ANY)
    inside = pl.BlockSpec(memory_space=pltpu.VMEM)
    left_out, bond_out = pl.pallas_call(
        kernel,
        out_shape=(
            pltpu.VMEM((2,) + block, f32),
            pltpu.VMEM(block, f32),
        ),
        in_specs=[pl.BlockSpec(memory_space=pltpu.SMEM)] + [pl.BlockSpec(memory_space=pltpu.HBM)] * 3,
        out_specs=(inside, inside),
        scratch_shapes=[
            pltpu.VMEM((2,) + block, f32),
            pltpu.VMEM(block, f32),
            pltpu.VMEM((channels,) + block, f32),
            pltpu.VMEM((channels,) + block, f32),
            pltpu.VMEM((2, channels) + block, bf16),
            pltpu.VMEM((2, channels) + block, bf16),
            pltpu.VMEM((states, 2 * states), f32),
            pltpu.VMEM((states, 2 * states), f32),
            pltpu.VMEM(block, f32),
            pltpu.VMEM(block, f32),
            pltpu.VMEM(block, f32),
            pltpu.VMEM(block, f32),
            pltpu.VMEM((2, 2) + block, f32),
            pltpu.VMEM((3, 2) + block, bf16),
            pltpu.VMEM((2, count, 16, 128), f32),
            pltpu.VMEM((2, 16, 128), f32),
            pltpu.SemaphoreType.DMA((3,)),
            pltpu.SemaphoreType.DMA((W_DN + W_UP + 6,)),
            pltpu.SemaphoreType.DMA((W_DN + W_UP + 6,)),
            pltpu.SemaphoreType.DMA((2, count)),
            pltpu.SemaphoreType.DMA((2, count)),
        ],
        compiler_params=pltpu.CompilerParams(
            collective_id=0, has_side_effects=True, vmem_limit_bytes=60 * 1024 * 1024
        ),
        name="bond_update",
    )(sector_size, site_tensor, left_env, right_env)
    return pl.pallas_call(
        write_out,
        out_shape=(
            jax.ShapeDtypeStruct(site_tensor.shape, f32),
            jax.ShapeDtypeStruct((1,) + block, f32),
        ),
        in_specs=[inside, inside],
        out_specs=(anywhere, anywhere),
        scratch_shapes=[pltpu.SemaphoreType.DMA((2,))],
        compiler_params=pltpu.CompilerParams(vmem_limit_bytes=4 * 1024 * 1024),
        name="write_out",
    )(left_out, bond_out)


def solution(mesh):
    placed = (
        P(("real", "row"), None, None, None),
        P(("real", "row"), None, None, None),
        P(("real", "row"), None, None, None),
        P("real"),
    )
    return jax.shard_map(
        on_device,
        mesh=mesh,
        in_specs=placed,
        out_specs=(P(("real", "row"), None, None, None), P(("real", "row"), None, None)),
        check_vma=False,
    )
```

profile of v0, /device:TPU:0, one launch (start us, length us, event | category | flops | bytes accessed | tf_op | source)
XLA Modules:
  0.0 58.7 jit_solution(12437085581497293654)
XLA Ops:
  0.6 57.2 %bond_update.1 = (f32[2,256,256]{2,1,0:T(8,128)S(1)}, f32[256,256]{1,0:T(8,128)S(1)}) custom-call(s32[16]{0:T(128)} %size_ref.1, f32[1,2,256,256]{3,2,1,0:T(8,128)} %site_hbm.1, f32[1,14,256,256]{3,2,1,0:T(8,128)} %left_hbm.1, f32[1,14,256,256]{3,2,1,0:T(8,128)} %right_hbm.1), custom_call_target="tpu_custom_call" | custom-call | tf_op jit(solution)/shard_map/bond_update/pallas_call | solution.py:383
  57.8 0.9 %write_out.1 = (f32[1,2,256,256]{3,2,1,0:T(8,128)}, f32[1,256,256]{2,1,0:T(8,128)}) custom-call(f32[2,256,256]{2,1,0:T(8,128)S(1)} %get-tuple-element.4.left, f32[256,256]{1,0:T(8,128)S(1)} %get-tuple-element.5.bond), custom_call_target="tpu_custom_call" | custom-call | tf_op jit(solution)/shard_map/write_out/pallas_call | solution.py:419
where the time goes:
time: 58.9 us; the launch traced here: 58.7 us
  Pallas kernels  58.1 us (99%)
  between operations  0.64 us (1%)
    pallas_call x1, Pallas kernels, on_device(): pl.pallas_call(kernel, out_shape=(pltpu.VMEM((2,) + block, f32), pltpu.VM...  57.2 us

commit v1 on v0

v1 whole, which is shorter than its diff:
```python
import jax
import jax.numpy as jnp
from jax import lax
from jax.experimental import pallas as pl
from jax.experimental.pallas import tpu as pltpu
from jax.sharding import PartitionSpec as P

SIDE = 4
EARLY = 3
PANEL = 16
TAU = 0.15
highest = lax.Precision.HIGHEST
f32 = jnp.float32
bf16 = jnp.bfloat16
MESH = pl.DeviceIdType.MESH


def dot(a, b):
    return jnp.dot(a, b, preferred_element_type=f32)


def exact_dot(a, b, dims):
    return lax.dot_general(a, b, (dims, ((), ())), precision=highest, preferred_element_type=f32)


def split_2(value):
    high = value.astype(bf16)
    return high, (value - high.astype(f32)).astype(bf16)


def split_3(value):
    high = value.astype(bf16)
    rest = value - high.astype(f32)
    middle = rest.astype(bf16)
    return high, middle, (rest - middle.astype(f32)).astype(bf16)


def store_split(pair_ref, index, value):
    high, low = split_2(value)
    pair_ref[0, index] = high
    pair_ref[1, index] = low


def row_sum(value):
    rows, columns = value.shape
    summed = jnp.sum(value.reshape(rows // 8, 8, columns), axis=0)
    total = summed[:, :128]
    for start in range(128, columns, 128):
        total = total + summed[:, start : start + 128]
    return jnp.sum(total, axis=0, keepdims=True)


def square(top_left, top_right, bottom_left, bottom_right):
    top = jnp.concatenate([top_left, top_right], 1)
    return jnp.concatenate([top, jnp.concatenate([bottom_left, bottom_right], 1)], 0)


def panel_step(p, lo, hi, states, aug_ref, out_ref):
    base = pl.multiple_of(p * PANEL, PANEL)
    row_id = lax.broadcasted_iota(jnp.int32, (PANEL, 128), 0)
    offset = lax.rem(p * PANEL, 128)
    diag = aug_ref[pl.ds(base, PANEL), lo : lo + 128]
    diag = pltpu.roll(diag, lax.rem(128 - offset, 128), 1)
    columns = [jnp.broadcast_to(diag[:, r : r + 1], (PANEL, 128)) for r in range(PANEL)]
    tiles = [aug_ref[pl.ds(base, PANEL), t : t + 128] for t in range(lo, hi, 128)]
    scale = jnp.zeros((PANEL, 128), f32)
    for r in range(PANEL):
        inverse = lax.rsqrt(columns[r][r : r + 1, :])
        scale = jnp.where(row_id == r, inverse, scale)
        multiplier = columns[r] * inverse
        below = jnp.where(row_id > r, multiplier, 0.0)
        for s in range(r + 1, PANEL):
            columns[s] = columns[s] - below * multiplier[s : s + 1, :]
        if r < PANEL - 1:
            tiles = [tile - below * (tile[r : r + 1, :] * inverse) for tile in tiles]
    tiles = [tile * scale for tile in tiles]
    for t, tile in zip(range(lo, hi, 128), tiles):
        out_ref[pl.ds(base, PANEL), t : t + 128] = tile
    panel = jnp.concatenate(tiles, 1)
    q1, q2, q3 = split_3(panel)
    p1, p2, p3 = (q[:, : states - lo] for q in (q1, q2, q3))
    left = jnp.concatenate([p1, p1, p2, p2, p1, p3], 0)
    right = jnp.concatenate([q1, q2, q1, q2, q3, q1], 0)
    update = lax.dot_general(left, right, (((0,), (0,)), ((), ())), preferred_element_type=f32)
    aug_ref[lo:states, lo:hi] -= update


def kernel(
    size_ref, site_hbm, left_hbm, right_hbm,
    left_out, bond_out,
    site, gram_own, gram_in, left_f, right_f, left_s, right_s, aug, fac, bond_own, bond_in, inv_own, inv_in,
    bond, applied, applied_in, acc, field_s, red_in, red_own, local_sem, send_sem, recv_sem, red_send, red_recv,
):
    count = lax.axis_size("row")
    me = lax.axis_index("row")
    states = site.shape[-1]
    half = states // 2
    channels = left_f.shape[0]
    moved = 2 * SIDE
    not_first, not_last = me > 0, me < count - 1
    to_right, to_left = jnp.minimum(me + 1, count - 1), jnp.maximum(me - 1, 0)

    loads = [
        pltpu.make_async_copy(site_hbm.at[0], site, local_sem.at[0]),
        pltpu.make_async_copy(left_hbm.at[0], left_f, local_sem.at[1]),
        pltpu.make_async_copy(right_hbm.at[0, moved:], right_f.at[moved:], local_sem.at[2]),
    ]
    for load in loads:
        load.start()

    barrier = pltpu.get_barrier_semaphore()
    for step in range(1, count):
        peer = lax.rem(me + step, count)
        pl.semaphore_signal(barrier, inc=1, device_id={"row": peer}, device_id_type=MESH)

    def remote(source, target, slot, peer):
        return pltpu.make_async_remote_copy(
            src_ref=source, dst_ref=target, send_sem=send_sem.at[slot], recv_sem=recv_sem.at[slot],
            device_id={"row": peer}, device_id_type=MESH,
        )

    gram_slot, bond_slot, applied_slot, inv_slot = moved, moved + 1, moved + 3, moved + 5
    send_gram = remote(gram_own, gram_in, gram_slot, to_right)
    send_down = [remote(right_hbm.at[0, a], right_f.at[a], a, to_right) for a in range(SIDE)]
    send_up = [remote(right_hbm.at[0, a], right_f.at[a], a, to_left) for a in range(SIDE, moved)]
    send_bond = [remote(bond_own, bond_in.at[s], bond_slot + s, (to_right, to_left)[s]) for s in range(2)]
    send_applied = [remote(applied, applied_in.at[s], applied_slot + s, (to_right, to_left)[s]) for s in range(2)]
    send_inv = remote(inv_own, inv_in, inv_slot, to_left)

    size = size_ref[me]
    size_before = size_ref[to_left]
    size_after = size_ref[to_right]
    row = lax.broadcasted_iota(jnp.int32, (states, states), 0)
    column = lax.broadcasted_iota(jnp.int32, (states, states), 1)
    block_row, block_column = row[:half, :half], column[:half, :half]
    on_diagonal = block_row == block_column
    live_pair = (row < size) & (column < size)

    @pl.when(me == 0)
    def _():
        gram_in[...] = jnp.zeros_like(gram_in)
        right_f[:SIDE] = jnp.zeros((SIDE, states, states), f32)
        bond_in[0] = jnp.zeros(bond_in.shape[1:], f32)
        applied_in[0] = jnp.zeros((states, states), f32)

    @pl.when(me == count - 1)
    def _():
        right_f[SIDE:moved] = jnp.zeros((SIDE, states, states), f32)
        bond_in[1] = jnp.zeros(bond_in.shape[1:], f32)
        applied_in[1] = jnp.zeros((states, states), f32)
        inv_in[...] = jnp.zeros_like(inv_in)

    def diagonal_rows(block):
        values = jnp.sum(jnp.where(on_diagonal, block, 0.0), axis=0, keepdims=True)
        return jnp.broadcast_to(values, (8, half))

    def store_packed(packed_ref, block, right_block, diagonal):
        packed_ref[:half, :half] = block
        packed_ref[:half, half:] = right_block
        packed_ref[half:, :half] = diagonal
        packed_ref[half:, half:] = diagonal

    loads[0].wait()
    gram_dims = ((0,), (0,))
    outer = jnp.where((row < size) & (column < size_after), site[1], 0.0)
    gram = exact_dot(outer, outer, gram_dims)
    store_packed(
        gram_own, jnp.where(block_column >= block_row, gram[:half, :half], gram[half:, half:]),
        gram[:half, half:], diagonal_rows(gram[half:, half:]),
    )
    pl.semaphore_wait(barrier, count - 1)

    @pl.when(not_last)
    def _():
        send_gram.start()

    upper = jnp.where(live_pair, site[0], 0.0)
    site[0] = upper
    gram = exact_dot(upper, upper, gram_dims)
    gram = gram + jnp.where((row == column) & (row >= size), 1.0, 0.0)
    aug[:, states:] = jnp.where(row == column, 1.0, 0.0).astype(f32)
    fac[...] = jnp.zeros_like(fac)

    @pl.when(not_last)
    def _():
        send_gram.wait_send()
        for one in send_down[:EARLY]:
            one.start()


    @pl.when(not_first)
    def _():
        send_gram.wait_recv()
        for one in send_up[:EARLY]:
            one.start()

    block = gram_in[:half, :half]
    mirrored = block.T
    top_left = jnp.where(block_column >= block_row, block, mirrored)
    bottom_right = jnp.where(block_column < block_row, block, jnp.where(on_diagonal, gram_in[half : half + 1, :half], mirrored))
    aug[:half, :half] = gram[:half, :half] + top_left
    aug[:half, half:states] = gram[:half, half:] + gram_in[:half, half:]
    aug[half:, :half] = gram[half:, :half]
    aug[half:, half:states] = gram[half:, half:] + bottom_right
    loads[1].wait()
    loads[2].wait()

    halves = half // PANEL

    def first_half(p, carry):
        panel_step(p, 0, states + half, states, aug, fac)
        store_split(left_s, p, left_f[p])
        return carry

    def second_half(p, carry):
        panel_step(p, half, 2 * states, states, aug, fac)
        other = jnp.minimum(p, channels - 1)
        store_split(left_s, other, left_f[other])
        mine = jnp.minimum(p - halves + moved, channels - 1)
        store_split(right_s, mine, right_f[mine])
        return carry

    lax.fori_loop(0, halves, first_half, 0)
    lax.fori_loop(halves, 2 * halves, second_half, 0)

    bottom_right = fac[half:, half:states]
    store_packed(
        bond_own, jnp.where(block_column >= block_row, fac[:half, :half], bottom_right.T),
        fac[:half, half:states], diagonal_rows(bottom_right),
    )

    @pl.when(not_last)
    def _():
        for one in [send_bond[0]] + send_down[EARLY:]:
            one.start()

    @pl.when(not_first)
    def _():
        for one in [send_bond[1]] + send_up[EARLY:]:
            one.start()

    bond[...] = jnp.where(live_pair & (column >= row), fac[:, :states], 0.0)

    def put_field(which, value):
        field_s[which, 0], field_s[which, 1] = split_2(value)

    def add_terms(total, which, a):
        high, low_part = field_s[which, 0], field_s[which, 1]
        r_high, r_low = right_s[0, a], right_s[1, a]
        l_high, l_low = left_s[0, a], left_s[1, a]
        middle = dot(high, r_high) + dot(high, r_low) + dot(low_part, r_high)
        m_high, m_low = split_2(middle)
        return total + dot(l_high, m_high) + dot(l_high, m_low) + dot(l_low, m_high)

    def add_range(which, start, amount):
        group = 2 if amount % 2 == 0 else 1

        def some(g, carry):
            total = acc[...]
            for k in range(group):
                total = add_terms(total, which, start + g * group + k)
            acc[...] = total
            return carry

        lax.fori_loop(0, amount // group, some, 0)

    near = 1 - lax.rem(me, 2)
    has_side = [jnp.where(s == 0, not_first, not_last) for s in (near, 1 - near)]
    sides = list(zip((near, 1 - near), has_side))

    acc[...] = jnp.zeros_like(acc)
    put_field(0, bond[...])
    add_range(0, moved, channels - moved)
    inverse = jnp.where(column <= row, fac[:, states:], 0.0)
    turned = ((1,), (1,))
    left_out[0] = exact_dot(site[0], inverse, turned)
    inv_own[:, :half] = jnp.where(block_column < block_row, inverse[:half, :half], inverse[half:, half:].T)
    inv_own[:, half:] = inverse[half:, :half]

    for order, (side, there) in enumerate(sides):

        @pl.when(there)
        def _():
            remote(bond_own, bond_in.at[side], bond_slot + side, to_right).wait_recv()

        limit = jnp.where(side == 0, size_before, size_after)
        block = bond_in[side, :half, :half]
        top_left = jnp.where(block_column >= block_row, block, 0.0)
        bottom_right = jnp.where(block_column > block_row, block.T, jnp.where(on_diagonal, bond_in[side, half : half + 1, :half], 0.0))
        field = square(top_left, bond_in[side, :half, half:], jnp.zeros((half, half), f32), bottom_right)
        put_field(1 + side, jnp.where((row < limit) & (column < limit), field, 0.0))

        def side_channel(k, carry, side=side, there=there):
            a = side * SIDE + k

            @pl.when(there)
            def _():
                remote(applied, right_f.at[a], a, to_right).wait_recv()

            store_split(right_s, a, right_f[a])
            acc[...] = add_terms(acc[...], 1 + side, a)
            return carry

        lax.fori_loop(0, EARLY, side_channel, 0)
        lax.fori_loop(EARLY, SIDE, side_channel, 0)

    def reductions(t):
        for step in range(1, count):
            peer = lax.rem(me + step, count)
            yield pltpu.make_async_remote_copy(
                src_ref=red_own.at[t], dst_ref=red_in.at[t, step],
                send_sem=red_send.at[t, step], recv_sem=red_recv.at[t, step],
                device_id={"row": peer}, device_id_type=MESH,
            )

    applied[...] = jnp.where(live_pair, acc[...], 0.0)

    @pl.when(not_last)
    def _():
        send_applied[0].start()

    @pl.when(not_first)
    def _():
        send_applied[1].start()
        send_inv.start()

    red_own[0, :1] = row_sum(bond[...] * bond[...])
    red_own[0, 1:] = row_sum(bond[...] * applied[...])
    first_sums = list(reductions(0))
    for one in first_sums:
        one.start()

    acc[...] = jnp.zeros_like(acc)
    put_field(0, applied[...])
    add_range(0, moved, channels - moved)

    for order, (side, there) in enumerate(sides):

        @pl.when(there)
        def _():
            remote(applied, applied_in.at[side], applied_slot + side, to_right).wait_recv()

        put_field(1 + side, applied_in[side])
        add_range(1 + side, side * SIDE, SIDE)

    def collect(t, copies):
        total = red_own[t]
        for step, one in enumerate(copies, 1):
            one.wait_recv()
            total = total + red_in[t, step]
        return jnp.sum(total, axis=1, keepdims=True)

    total = collect(0, first_sums)
    start_norm = total[:1]
    energy = total[1:] / start_norm
    shifted = applied[...] - energy * bond[...]
    second = jnp.where(live_pair, acc[...], 0.0) - energy * applied[...] - energy * shifted
    acc[...] = bond[...] + TAU * shifted + (0.5 * TAU * TAU) * second
    red_own[1, :1] = row_sum(acc[...] * acc[...])
    red_own[1, 1:] = jnp.zeros((1, 128), f32)
    second_sums = list(reductions(1))
    for one in second_sums:
        one.start()


    @pl.when(not_last)
    def _():
        send_inv.wait_recv()

    block = inv_in[:, :half]
    near_block, near_low = bond_in[1, :half, :half], bond_in[1, half : half + 1, :half]
    zeros = jnp.zeros((half, half), f32)
    top_left = jnp.where(block_column < block_row, block, jnp.where(on_diagonal, 1.0 / near_block, 0.0))
    bottom_right = jnp.where(block_column < block_row, block.T, jnp.where(on_diagonal, 1.0 / near_low, 0.0))
    outer = jnp.where((row < size) & (column < size_after), site[1], 0.0)
    outer = exact_dot(outer, square(top_left, zeros, inv_in[:, half:], bottom_right), turned)
    left_out[1] = jnp.where(not_last, outer, 0.0)

    @pl.when(not_last)
    def _():
        for one in send_down + [send_bond[0], send_applied[0]]:
            one.wait_send()

    @pl.when(not_first)
    def _():
        for one in send_up + [send_bond[1], send_applied[1], send_inv]:
            one.wait_send()

    final_norm = collect(1, second_sums)[:1]
    bond_out[...] = acc[...] * jnp.sqrt(start_norm / final_norm)
    for one in first_sums + second_sums:
        one.wait_send()


def write_out(left, bond, left_hbm, bond_hbm, sem):
    stores = [
        pltpu.make_async_copy(left, left_hbm.at[0], sem.at[0]),
        pltpu.make_async_copy(bond, bond_hbm.at[0], sem.at[1]),
    ]
    for store in stores:
        store.start()
    for store in stores:
        store.wait()


def on_device(site_tensor, left_env, right_env, sector_size):
    states = site_tensor.shape[-1]
    channels = left_env.shape[1]
    count = lax.axis_size("row")
    block = (states, states)
    triangle = (states // 2 + 8, states)
    slots = 2 * SIDE + 6
    anywhere = pl.BlockSpec(memory_space=pl.ANY)
    inside = pl.BlockSpec(memory_space=pltpu.VMEM)
    left_out, bond_out = pl.pallas_call(
        kernel,
        out_shape=(
            pltpu.VMEM((2,) + block, f32),
            pltpu.VMEM(block, f32),
        ),
        in_specs=[pl.BlockSpec(memory_space=pltpu.SMEM)] + [pl.BlockSpec(memory_space=pltpu.HBM)] * 3,
        out_specs=(inside, inside),
        scratch_shapes=[
            pltpu.VMEM((2,) + block, f32),
            pltpu.VMEM(triangle, f32),
            pltpu.VMEM(triangle, f32),
            pltpu.VMEM((channels,) + block, f32),
            pltpu.VMEM((channels,) + block, f32),
            pltpu.VMEM((2, channels) + block, bf16),
            pltpu.VMEM((2, channels) + block, bf16),
            pltpu.VMEM((states, 2 * states), f32),
            pltpu.VMEM((states, 2 * states), f32),
            pltpu.VMEM(triangle, f32),
            pltpu.VMEM((2,) + triangle, f32),
            pltpu.VMEM((states // 2, states), f32),
            pltpu.VMEM((states // 2, states), f32),
            pltpu.VMEM(block, f32),
            pltpu.VMEM(block, f32),
            pltpu.VMEM((2,) + block, f32),
            pltpu.VMEM(block, f32),
            pltpu.VMEM((3, 2) + block, bf16),
            pltpu.VMEM((2, count, 2, 128), f32),
            pltpu.VMEM((2, 2, 128), f32),
            pltpu.SemaphoreType.DMA((3,)),
            pltpu.SemaphoreType.DMA((slots,)),
            pltpu.SemaphoreType.DMA((slots,)),
            pltpu.SemaphoreType.DMA((2, count)),
            pltpu.SemaphoreType.DMA((2, count)),
        ],
        compiler_params=pltpu.CompilerParams(
            collective_id=0, has_side_effects=True, vmem_limit_bytes=60 * 1024 * 1024
        ),
        name="bond_update",
    )(sector_size, site_tensor, left_env, right_env)
    return pl.pallas_call(
        write_out,
        out_shape=(
            jax.ShapeDtypeStruct(site_tensor.shape, f32),
            jax.ShapeDtypeStruct((1,) + block, f32),
        ),
        in_specs=[inside, inside],
        out_specs=(anywhere, anywhere),
        scratch_shapes=[pltpu.SemaphoreType.DMA((2,))],
        compiler_params=pltpu.CompilerParams(vmem_limit_bytes=4 * 1024 * 1024),
        name="write_out",
    )(left_out, bond_out)


def solution(mesh):
    placed = (
        P(("real", "row"), None, None, None),
        P(("real", "row"), None, None, None),
        P(("real", "row"), None, None, None),
        P("real"),
    )
    return jax.shard_map(
        on_device,
        mesh=mesh,
        in_specs=placed,
        out_specs=(P(("real", "row"), None, None, None), P(("real", "row"), None, None)),
        check_vma=False,
    )
```

time: 58.9 us -> 53.6 us (0.910)
  Pallas kernels: 58.1 us -> 52.8 us
    pallas_call x1, Pallas kernels: 57.2 us -> 51.9 us  [on_device(): pl.pallas_call(kernel, out_shape=(pltpu.VMEM((2,) + block, f32), pltpu.VM...]
where the time goes in v1:
time: 53.6 us; the launch traced here: 53.5 us
  Pallas kernels  52.8 us (99%)
  between operations  0.64 us (1%)
    pallas_call x1, Pallas kernels, on_device(): pl.pallas_call(kernel, out_shape=(pltpu.VMEM((2,) + block, f32), pltpu.VM...  51.9 us

profile of v1, /device:TPU:0, one launch (start us, length us, event | category | flops | bytes accessed | tf_op | source)
XLA Modules:
  0.0 53.5 jit_solution(9608441332229474929)
XLA Ops:
  0.6 51.9 %bond_update.1 = (f32[2,256,256]{2,1,0:T(8,128)S(1)}, f32[256,256]{1,0:T(8,128)S(1)}) custom-call(s32[16]{0:T(128)} %size_ref.1, f32[1,2,256,256]{3,2,1,0:T(8,128)} %site_hbm.1, f32[1,14,256,256]{3,2,1,0:T(8,128)} %left_hbm.1, f32[1,14,256,256]{3,2,1,0:T(8,128)} %right_hbm.1), custom_call_target="tpu_custom_call" | custom-call | tf_op jit(solution)/shard_map/bond_update/pallas_call | solution.py:415
  52.6 0.9 %write_out.1 = (f32[1,2,256,256]{3,2,1,0:T(8,128)}, f32[1,256,256]{2,1,0:T(8,128)}) custom-call(f32[2,256,256]{2,1,0:T(8,128)S(1)} %get-tuple-element.4.left, f32[256,256]{1,0:T(8,128)S(1)} %get-tuple-element.5.bond), custom_call_target="tpu_custom_call" | custom-call | tf_op jit(solution)/shard_map/write_out/pallas_call | solution.py:455

commit v2 on v1

--- a/solution.py
+++ b/solution.py
@@ -86,9 +86,9 @@
 
 
 def kernel(
-    size_ref, site_hbm, left_hbm, right_hbm,
+    size_hbm, site_hbm, left_hbm, right_hbm,
     left_out, bond_out,
-    site, gram_own, gram_in, left_f, right_f, left_s, right_s, aug, fac, bond_own, bond_in, inv_own, inv_in,
+    size_ref, site, gram_own, gram_in, left_f, right_f, left_s, right_s, aug, fac, bond_own, bond_in, inv_own, inv_in,
     bond, applied, applied_in, acc, field_s, red_in, red_own, local_sem, send_sem, recv_sem, red_send, red_recv,
 ):
     count = lax.axis_size("row")
@@ -105,6 +105,8 @@
         pltpu.make_async_copy(left_hbm.at[0], left_f, local_sem.at[1]),
         pltpu.make_async_copy(right_hbm.at[0, moved:], right_f.at[moved:], local_sem.at[2]),
     ]
+    load_size = pltpu.make_async_copy(size_hbm, size_ref, local_sem.at[3])
+    load_size.start()
     for load in loads:
         load.start()
 
@@ -113,20 +115,44 @@
         peer = lax.rem(me + step, count)
         pl.semaphore_signal(barrier, inc=1, device_id={"row": peer}, device_id_type=MESH)
 
-    def remote(source, target, slot, peer):
+    def remote(source, target, sent, received, peer):
         return pltpu.make_async_remote_copy(
-            src_ref=source, dst_ref=target, send_sem=send_sem.at[slot], recv_sem=recv_sem.at[slot],
+            src_ref=source, dst_ref=target, send_sem=send_sem.at[sent], recv_sem=recv_sem.at[received],
             device_id={"row": peer}, device_id_type=MESH,
         )
 
-    gram_slot, bond_slot, applied_slot, inv_slot = moved, moved + 1, moved + 3, moved + 5
-    send_gram = remote(gram_own, gram_in, gram_slot, to_right)
-    send_down = [remote(right_hbm.at[0, a], right_f.at[a], a, to_right) for a in range(SIDE)]
-    send_up = [remote(right_hbm.at[0, a], right_f.at[a], a, to_left) for a in range(SIDE, moved)]
-    send_bond = [remote(bond_own, bond_in.at[s], bond_slot + s, (to_right, to_left)[s]) for s in range(2)]
-    send_applied = [remote(applied, applied_in.at[s], applied_slot + s, (to_right, to_left)[s]) for s in range(2)]
-    send_inv = remote(inv_own, inv_in, inv_slot, to_left)
-
+    halves = [slice(0, half), slice(half, states)]
+    peers = (to_right, to_left)
+
+    def block_copy(side, k, peer):
+        a = side * SIDE + k
+        return remote(right_hbm.at[0, a], right_f.at[a], 1 + side, (1 if k < EARLY else 3) + side, peer)
+
+    def blocks_sent(side):
+        channels_of = pl.ds(side * SIDE, SIDE)
+        return remote(right_hbm.at[0, channels_of], right_f.at[channels_of], 1 + side, 1 + side, to_right)
+
+    def early_blocks(side):
+        channels_of = pl.ds(side * SIDE, EARLY)
+        return remote(right_hbm.at[0, channels_of], right_f.at[channels_of], 1 + side, 1 + side, to_right)
+
+    def bond_copy(side, peer):
+        return remote(bond_own, bond_in.at[side], 3 + side, 5 + side, peer)
+
+    def applied_copy(side, part, peer):
+        rows = halves[part]
+        return remote(applied.at[rows], applied_in.at[side, rows], 5 + side, 7 + 2 * side + part, peer)
+
+    def applied_sent(side):
+        return remote(applied, applied_in.at[side], 5 + side, 7 + 2 * side, to_right)
+
+    send_gram = remote(gram_own, gram_in, 0, 0, to_right)
+    send_inv = remote(inv_own, inv_in, 7, 11, to_left)
+    sends = [[block_copy(s, k, peers[s]) for k in range(SIDE)] for s in range(2)]
+    send_bond = [bond_copy(s, peers[s]) for s in range(2)]
+    send_applied = [[applied_copy(s, part, peers[s]) for part in range(2)] for s in range(2)]
+
+    load_size.wait()
     size = size_ref[me]
     size_before = size_ref[to_left]
     size_after = size_ref[to_right]
@@ -184,14 +210,14 @@
     @pl.when(not_last)
     def _():
         send_gram.wait_send()
-        for one in send_down[:EARLY]:
+        for one in sends[0][:EARLY]:
             one.start()
 
 
     @pl.when(not_first)
     def _():
         send_gram.wait_recv()
-        for one in send_up[:EARLY]:
+        for one in sends[1][:EARLY]:
             one.start()
 
     block = gram_in[:half, :half]
@@ -205,7 +231,7 @@
     loads[1].wait()
     loads[2].wait()
 
-    halves = half // PANEL
+    panels = half // PANEL
 
     def first_half(p, carry):
         panel_step(p, 0, states + half, states, aug, fac)
@@ -216,12 +242,12 @@
         panel_step(p, half, 2 * states, states, aug, fac)
         other = jnp.minimum(p, channels - 1)
         store_split(left_s, other, left_f[other])
-        mine = jnp.minimum(p - halves + moved, channels - 1)
+        mine = jnp.minimum(p - panels + moved, channels - 1)
         store_split(right_s, mine, right_f[mine])
         return carry
 
-    lax.fori_loop(0, halves, first_half, 0)
-    lax.fori_loop(halves, 2 * halves, second_half, 0)
+    lax.fori_loop(0, panels, first_half, 0)
+    lax.fori_loop(panels, 2 * panels, second_half, 0)
 
     bottom_right = fac[half:, half:states]
     store_packed(
@@ -231,12 +257,12 @@
 
     @pl.when(not_last)
     def _():
-        for one in [send_bond[0]] + send_down[EARLY:]:
+        for one in [send_bond[0]] + sends[0][EARLY:]:
             one.start()
 
     @pl.when(not_first)
     def _():
-        for one in [send_bond[1]] + send_up[EARLY:]:
+        for one in [send_bond[1]] + sends[1][EARLY:]:
             one.start()
 
     bond[...] = jnp.where(live_pair & (column >= row), fac[:, :states], 0.0)
@@ -244,13 +270,17 @@
     def put_field(which, value):
         field_s[which, 0], field_s[which, 1] = split_2(value)
 
+    def middle_of(which, a, rows):
+        high, low_part = field_s[which, 0, rows], field_s[which, 1, rows]
+        r_high, r_low = right_s[0, a], right_s[1, a]
+        return split_2(dot(high, r_high) + dot(high, r_low) + dot(low_part, r_high))
+
+    def outside(total, l_high, l_low, m_high, m_low):
+        return total + dot(l_high, m_high) + dot(l_high, m_low) + dot(l_low, m_high)
+
     def add_terms(total, which, a):
-        high, low_part = field_s[which, 0], field_s[which, 1]
-        r_high, r_low = right_s[0, a], right_s[1, a]
-        l_high, l_low = left_s[0, a], left_s[1, a]
-        middle = dot(high, r_high) + dot(high, r_low) + dot(low_part, r_high)
-        m_high, m_low = split_2(middle)
-        return total + dot(l_high, m_high) + dot(l_high, m_low) + dot(l_low, m_high)
+        m_high, m_low = middle_of(which, a, slice(None))
+        return outside(total, left_s[0, a], left_s[1, a], m_high, m_low)
 
     def add_range(which, start, amount):
         group = 2 if amount % 2 == 0 else 1
@@ -281,7 +311,7 @@
 
         @pl.when(there)
         def _():
-            remote(bond_own, bond_in.at[side], bond_slot + side, to_right).wait_recv()
+            bond_copy(side, to_right).wait_recv()
 
         limit = jnp.where(side == 0, size_before, size_after)
         block = bond_in[side, :half, :half]
@@ -290,67 +320,93 @@
         field = square(top_left, bond_in[side, :half, half:], jnp.zeros((half, half), f32), bottom_right)
         put_field(1 + side, jnp.where((row < limit) & (column < limit), field, 0.0))
 
-        def side_channel(k, carry, side=side, there=there):
-            a = side * SIDE + k
-
-            @pl.when(there)
-            def _():
-                remote(applied, right_f.at[a], a, to_right).wait_recv()
-
-            store_split(right_s, a, right_f[a])
-            acc[...] = add_terms(acc[...], 1 + side, a)
-            return carry
-
-        lax.fori_loop(0, EARLY, side_channel, 0)
-        lax.fori_loop(EARLY, SIDE, side_channel, 0)
+        @pl.when(there)
+        def _():
+            early_blocks(side).wait_recv()
+
+        for k in range(EARLY):
+            store_split(right_s, side * SIDE + k, right_f[side * SIDE + k])
+        total = acc[...]
+        for k in range(EARLY):
+            total = add_terms(total, 1 + side, side * SIDE + k)
+        acc[...] = total
+
+        @pl.when(there)
+        def _():
+            block_copy(side, EARLY, to_right).wait_recv()
+
+        last = side * SIDE + EARLY
+        store_split(right_s, last, right_f[last])
+        if order == 0:
+            acc[...] = add_terms(acc[...], 1 + side, last)
 
     def reductions(t):
         for step in range(1, count):
             peer = lax.rem(me + step, count)
             yield pltpu.make_async_remote_copy(
-                src_ref=red_own.at[t], dst_ref=red_in.at[t, step],
-                send_sem=red_send.at[t, step], recv_sem=red_recv.at[t, step],
+                src_ref=red_own.at[t], dst_ref=red_in.at[t, step - 1],
+                send_sem=red_send.at[t], recv_sem=red_recv.at[t],
                 device_id={"row": peer}, device_id_type=MESH,
             )
 
-    applied[...] = jnp.where(live_pair, acc[...], 0.0)
-
-    @pl.when(not_last)
-    def _():
-        send_applied[0].start()
-
-    @pl.when(not_first)
-    def _():
-        send_applied[1].start()
-        send_inv.start()
-
-    red_own[0, :1] = row_sum(bond[...] * bond[...])
-    red_own[0, 1:] = row_sum(bond[...] * applied[...])
-    first_sums = list(reductions(0))
-    for one in first_sums:
-        one.start()
+    def all_reductions(t):
+        return pltpu.make_async_remote_copy(
+            src_ref=red_in.at[t], dst_ref=red_in.at[t], send_sem=red_send.at[t], recv_sem=red_recv.at[t],
+            device_id={"row": to_right}, device_id_type=MESH,
+        )
+
+    last = (1 - near) * SIDE + EARLY
+    m_high, m_low = middle_of(2 - near, last, slice(None))
+    for part, rows in enumerate(halves):
+        value = outside(acc[rows], left_s[0, last, rows], left_s[1, last, rows], m_high, m_low)
+        applied[rows] = jnp.where(live_pair[rows], value, 0.0)
+        if part == 1:
+            red_own[0, :1] = row_sum(bond[...] * bond[...])
+            red_own[0, 1:] = row_sum(bond[...] * applied[...])
+            for one in reductions(0):
+                one.start()
+
+        @pl.when(not_last)
+        def _():
+            send_applied[0][part].start()
+
+        @pl.when(not_first)
+        def _():
+            send_applied[1][part].start()
 
     acc[...] = jnp.zeros_like(acc)
     put_field(0, applied[...])
     add_range(0, moved, channels - moved)
 
     for order, (side, there) in enumerate(sides):
-
-        @pl.when(there)
-        def _():
-            remote(applied, applied_in.at[side], applied_slot + side, to_right).wait_recv()
-
-        put_field(1 + side, applied_in[side])
-        add_range(1 + side, side * SIDE, SIDE)
-
-    def collect(t, copies):
-        total = red_own[t]
-        for step, one in enumerate(copies, 1):
-            one.wait_recv()
-            total = total + red_in[t, step]
-        return jnp.sum(total, axis=1, keepdims=True)
-
-    total = collect(0, first_sums)
+        for part, rows in enumerate(halves):
+
+            @pl.when(there)
+            def _():
+                applied_copy(side, part, to_right).wait_recv()
+
+            if order == 0 and part == 1:
+
+                @pl.when(not_first)
+                def _():
+                    send_inv.start()
+
+            which = 1 + side
+            field_s[which, 0, rows], field_s[which, 1, rows] = split_2(applied_in[side, rows])
+            middles = [middle_of(which, side * SIDE + k, rows) for k in range(SIDE)]
+            total = acc[...]
+            for k in range(0, SIDE, 2):
+                pair = [side * SIDE + k, side * SIDE + k + 1]
+                l_high, l_low = (jnp.concatenate([left_s[i, a, :, rows] for a in pair], 1) for i in range(2))
+                m_high, m_low = (jnp.concatenate([middles[k + j][i] for j in range(2)], 0) for i in range(2))
+                total = outside(total, l_high, l_low, m_high, m_low)
+            acc[...] = total
+
+    def collect(t):
+        all_reductions(t).wait_recv()
+        return jnp.sum(red_own[t] + jnp.sum(red_in[t], axis=0), axis=1, keepdims=True)
+
+    total = collect(0)
     start_norm = total[:1]
     energy = total[1:] / start_norm
     shifted = applied[...] - energy * bond[...]
@@ -358,8 +414,7 @@
     acc[...] = bond[...] + TAU * shifted + (0.5 * TAU * TAU) * second
     red_own[1, :1] = row_sum(acc[...] * acc[...])
     red_own[1, 1:] = jnp.zeros((1, 128), f32)
-    second_sums = list(reductions(1))
-    for one in second_sums:
+    for one in reductions(1):
         one.start()
 
 
@@ -378,18 +433,18 @@
 
     @pl.when(not_last)
     def _():
-        for one in send_down + [send_bond[0], send_applied[0]]:
+        for one in [blocks_sent(0), send_bond[0], applied_sent(0)]:
             one.wait_send()
 
     @pl.when(not_first)
     def _():
-        for one in send_up + [send_bond[1], send_applied[1], send_inv]:
+        for one in [blocks_sent(1), send_bond[1], applied_sent(1), send_inv]:
             one.wait_send()
 
-    final_norm = collect(1, second_sums)[:1]
+    final_norm = collect(1)[:1]
     bond_out[...] = acc[...] * jnp.sqrt(start_norm / final_norm)
-    for one in first_sums + second_sums:
-        one.wait_send()
+    for t in range(2):
+        all_reductions(t).wait_send()
 
 
 def write_out(left, bond, left_hbm, bond_hbm, sem):
@@ -409,7 +464,6 @@
     count = lax.axis_size("row")
     block = (states, states)
     triangle = (states // 2 + 8, states)
-    slots = 2 * SIDE + 6
     anywhere = pl.BlockSpec(memory_space=pl.ANY)
     inside = pl.BlockSpec(memory_space=pltpu.VMEM)
     left_out, bond_out = pl.pallas_call(
@@ -418,9 +472,10 @@
             pltpu.VMEM((2,) + block, f32),
             pltpu.VMEM(block, f32),
         ),
-        in_specs=[pl.BlockSpec(memory_space=pltpu.SMEM)] + [pl.BlockSpec(memory_space=pltpu.HBM)] * 3,
+        in_specs=[pl.BlockSpec(memory_space=pltpu.HBM)] * 4,
         out_specs=(inside, inside),
         scratch_shapes=[
+            pltpu.SMEM(sector_size.shape, jnp.int32),
             pltpu.VMEM((2,) + block, f32),
             pltpu.VMEM(triangle, f32),
             pltpu.VMEM(triangle, f32),
@@ -439,13 +494,13 @@
             pltpu.VMEM((2,) + block, f32),
             pltpu.VMEM(block, f32),
             pltpu.VMEM((3, 2) + block, bf16),
-            pltpu.VMEM((2, count, 2, 128), f32),
+            pltpu.VMEM((2, count - 1, 2, 128), f32),
             pltpu.VMEM((2, 2, 128), f32),
-            pltpu.SemaphoreType.DMA((3,)),
-            pltpu.SemaphoreType.DMA((slots,)),
-            pltpu.SemaphoreType.DMA((slots,)),
-            pltpu.SemaphoreType.DMA((2, count)),
-            pltpu.SemaphoreType.DMA((2, count)),
+            pltpu.SemaphoreType.DMA((4,)),
+            pltpu.SemaphoreType.DMA((8,)),
+            pltpu.SemaphoreType.DMA((12,)),
+            pltpu.SemaphoreType.DMA((2,)),
+            pltpu.SemaphoreType.DMA((2,)),
         ],
         compiler_params=pltpu.CompilerParams(
             collective_id=0, has_side_effects=True, vmem_limit_bytes=60 * 1024 * 1024

time: 53.6 us -> 51.6 us (0.963)
  Pallas kernels: 52.8 us -> 50.8 us
    pallas_call x1, Pallas kernels: 51.9 us -> 49.9 us  [on_device(): pl.pallas_call(kernel, out_shape=(pltpu.VMEM((2,) + block, f32), pltpu.VM...]
where the time goes in v2:
time: 51.6 us; the launch traced here: 51.5 us
  Pallas kernels  50.8 us (98%)
  between operations  0.64 us (1%)
    pallas_call x1, Pallas kernels, on_device(): pl.pallas_call(kernel, out_shape=(pltpu.VMEM((2,) + block, f32), pltpu.VM...  49.9 us

profile of v2, /device:TPU:0, one launch (start us, length us, event | category | flops | bytes accessed | tf_op | source)
XLA Modules:
  0.0 51.5 jit_solution(1376066765611871472)
XLA Ops:
  0.6 49.9 %bond_update.1 = (f32[2,256,256]{2,1,0:T(8,128)S(1)}, f32[256,256]{1,0:T(8,128)S(1)}) custom-call(s32[16]{0:T(128)} %size_hbm.1, f32[1,2,256,256]{3,2,1,0:T(8,128)} %site_hbm.1, f32[1,14,256,256]{3,2,1,0:T(8,128)} %left_hbm.1, f32[1,14,256,256]{3,2,1,0:T(8,128)} %right_hbm.1), custom_call_target="tpu_custom_call" | custom-call | tf_op jit(solution)/shard_map/bond_update/pallas_call | solution.py:469
  50.6 0.9 %write_out.1 = (f32[1,2,256,256]{3,2,1,0:T(8,128)}, f32[1,256,256]{2,1,0:T(8,128)}) custom-call(f32[2,256,256]{2,1,0:T(8,128)S(1)} %get-tuple-element.4.left, f32[256,256]{1,0:T(8,128)S(1)} %get-tuple-element.5.bond), custom_call_target="tpu_custom_call" | custom-call | tf_op jit(solution)/shard_map/write_out/pallas_call | solution.py:510

commit v3 on v2

--- a/solution.py
+++ b/solution.py
@@ -7,6 +7,7 @@
 
 SIDE = 4
 EARLY = 3
+QUAD = 4
 PANEL = 16
 TAU = 0.15
 highest = lax.Precision.HIGHEST
@@ -89,7 +90,8 @@
     size_hbm, site_hbm, left_hbm, right_hbm,
     left_out, bond_out,
     size_ref, site, gram_own, gram_in, left_f, right_f, left_s, right_s, aug, fac, bond_own, bond_in, inv_own, inv_in,
-    bond, applied, applied_in, acc, field_s, red_in, red_own, local_sem, send_sem, recv_sem, red_send, red_recv,
+    bond, applied, applied_in, acc, field_s, red_in, red_own, relayed,
+    local_sem, send_sem, recv_sem, red_send, red_recv, relay_send, relay_recv, greetings,
 ):
     count = lax.axis_size("row")
     me = lax.axis_index("row")
@@ -111,9 +113,26 @@
         load.start()
 
     barrier = pltpu.get_barrier_semaphore()
-    for step in range(1, count):
-        peer = lax.rem(me + step, count)
-        pl.semaphore_signal(barrier, inc=1, device_id={"row": peer}, device_id_type=MESH)
+
+    def greet(semaphore, distance):
+        for there, peer in ((me >= distance, me - distance), (me < count - distance, me + distance)):
+
+            @pl.when(there)
+            def _():
+                pl.semaphore_signal(semaphore, inc=1, device_id={"row": peer}, device_id_type=MESH)
+
+    def greeted(semaphore, distance):
+        peers_of = jnp.where(me >= distance, 1, 0) + jnp.where(me < count - distance, 1, 0)
+        pl.semaphore_wait(semaphore, peers_of)
+
+    levels = (count - 1).bit_length()
+
+    def know(level):
+        greeted(greetings.at[level], 2**level)
+        if level + 1 < levels:
+            greet(greetings.at[level + 1], 2 ** (level + 1))
+
+    greet(barrier, 1)
 
     def remote(source, target, sent, received, peer):
         return pltpu.make_async_remote_copy(
@@ -145,6 +164,42 @@
 
     def applied_sent(side):
         return remote(applied, applied_in.at[side], 5 + side, 7 + 2 * side, to_right)
+
+    quads = count // QUAD
+    quad, place = me // QUAD, lax.rem(me, QUAD)
+    goes_up = quad * SIDE // quads if count % QUAD == 0 else 0 * quad
+    goes_down = SIDE - (quad + 1) * SIDE // quads if count % QUAD == 0 else 0 * quad
+    relays_up, relays_down = place == QUAD - 1, place == 0
+    by_relay = (jnp.where(relays_up, goes_down, 0), jnp.where(relays_down, goes_up, 0))
+    relay_amount = jnp.where(relays_up, goes_up, jnp.where(relays_down, goes_down, 0))
+    across = jnp.clip(jnp.where(relays_up, me - QUAD + 1, me + QUAD - 1), 0, count - 1)
+    beyond = jnp.clip(jnp.where(relays_up, me - QUAD, me + QUAD), 0, count - 1)
+    relay_side = jnp.where(relays_up, 1, 0)
+
+    def to_relay(side, k):
+        return pltpu.make_async_remote_copy(
+            src_ref=right_hbm.at[0, side * SIDE + k], dst_ref=relayed.at[k],
+            send_sem=send_sem.at[1 + side], recv_sem=relay_recv.at[k],
+            device_id={"row": across}, device_id_type=MESH,
+        )
+
+    def from_relay(k):
+        return pltpu.make_async_remote_copy(
+            src_ref=relayed.at[k], dst_ref=right_f.at[relay_side * SIDE + k],
+            send_sem=relay_send.at[k], recv_sem=recv_sem.at[1 + relay_side],
+            device_id={"row": beyond}, device_id_type=MESH,
+        )
+
+    def start_early(side):
+        for k in range(EARLY):
+
+            @pl.when(k < by_relay[side])
+            def _():
+                to_relay(side, k).start()
+
+            @pl.when(k >= by_relay[side])
+            def _():
+                sends[side][k].start()
 
     send_gram = remote(gram_own, gram_in, 0, 0, to_right)
     send_inv = remote(inv_own, inv_in, 7, 11, to_left)
@@ -194,7 +249,8 @@
         gram_own, jnp.where(block_column >= block_row, gram[:half, :half], gram[half:, half:]),
         gram[:half, half:], diagonal_rows(gram[half:, half:]),
     )
-    pl.semaphore_wait(barrier, count - 1)
+    greeted(barrier, 1)
+    greet(greetings.at[0], 1)
 
     @pl.when(not_last)
     def _():
@@ -206,19 +262,28 @@
     gram = gram + jnp.where((row == column) & (row >= size), 1.0, 0.0)
     aug[:, states:] = jnp.where(row == column, 1.0, 0.0).astype(f32)
     fac[...] = jnp.zeros_like(fac)
+    know(0)
 
     @pl.when(not_last)
     def _():
         send_gram.wait_send()
-        for one in sends[0][:EARLY]:
-            one.start()
+
+    know(1)
+
+    waits_down, waits_up = not_last & (place == 1), not_first & (place == 2)
+
+    @pl.when(not_last & ~waits_down)
+    def _():
+        start_early(0)
 
 
     @pl.when(not_first)
     def _():
         send_gram.wait_recv()
-        for one in sends[1][:EARLY]:
-            one.start()
+
+    @pl.when(not_first & ~waits_up)
+    def _():
+        start_early(1)
 
     block = gram_in[:half, :half]
     mirrored = block.T
@@ -247,7 +312,19 @@
         return carry
 
     lax.fori_loop(0, panels, first_half, 0)
+    know(2)
+
+    @pl.when(waits_down)
+    def _():
+        start_early(0)
+
+    @pl.when(waits_up)
+    def _():
+        start_early(1)
+
     lax.fori_loop(panels, 2 * panels, second_half, 0)
+    for level in range(3, levels):
+        know(level)
 
     bottom_right = fac[half:, half:states]
     store_packed(
@@ -267,6 +344,16 @@
 
     bond[...] = jnp.where(live_pair & (column >= row), fac[:, :states], 0.0)
 
+    def relay(start, stop):
+        for k in range(start, stop):
+
+            @pl.when(k < relay_amount)
+            def _():
+                to_relay(0, k).wait_recv()
+                from_relay(k).start()
+
+    relay(0, 2)
+
     def put_field(which, value):
         field_s[which, 0], field_s[which, 1] = split_2(value)
 
@@ -283,7 +370,7 @@
         return outside(total, left_s[0, a], left_s[1, a], m_high, m_low)
 
     def add_range(which, start, amount):
-        group = 2 if amount % 2 == 0 else 1
+        group = next(n for n in (3, 2, 1) if amount % n == 0)
 
         def some(g, carry):
             total = acc[...]
@@ -301,6 +388,7 @@
     acc[...] = jnp.zeros_like(acc)
     put_field(0, bond[...])
     add_range(0, moved, channels - moved)
+    relay(2, EARLY)
     inverse = jnp.where(column <= row, fac[:, states:], 0.0)
     turned = ((1,), (1,))
     left_out[0] = exact_dot(site[0], inverse, turned)
@@ -355,6 +443,7 @@
             device_id={"row": to_right}, device_id_type=MESH,
         )
 
+    held = (not_last & (place == QUAD - 1), not_first & (place == 0))
     last = (1 - near) * SIDE + EARLY
     m_high, m_low = middle_of(2 - near, last, slice(None))
     for part, rows in enumerate(halves):
@@ -366,17 +455,19 @@
             for one in reductions(0):
                 one.start()
 
-        @pl.when(not_last)
+        @pl.when(not_last & ~held[0])
         def _():
             send_applied[0][part].start()
 
-        @pl.when(not_first)
+        @pl.when(not_first & ~held[1])
         def _():
             send_applied[1][part].start()
 
     acc[...] = jnp.zeros_like(acc)
     put_field(0, applied[...])
-    add_range(0, moved, channels - moved)
+    first_own = (channels - moved) // 2
+    add_range(0, moved, first_own)
+    add_range(0, moved + first_own, channels - moved - first_own)
 
     for order, (side, there) in enumerate(sides):
         for part, rows in enumerate(halves):
@@ -385,7 +476,15 @@
             def _():
                 applied_copy(side, part, to_right).wait_recv()
 
-            if order == 0 and part == 1:
+            if order == 0 and part == 0:
+                for s in range(2):
+
+                    @pl.when(held[s])
+                    def _():
+                        for one in send_applied[s]:
+                            one.start()
+
+            if order == 1 and part == 1:
 
                 @pl.when(not_first)
                 def _():
@@ -440,6 +539,12 @@
     def _():
         for one in [blocks_sent(1), send_bond[1], applied_sent(1), send_inv]:
             one.wait_send()
+
+    for k in range(EARLY):
+
+        @pl.when(k < relay_amount)
+        def _():
+            from_relay(k).wait_send()
 
     final_norm = collect(1)[:1]
     bond_out[...] = acc[...] * jnp.sqrt(start_norm / final_norm)
@@ -496,11 +601,15 @@
             pltpu.VMEM((3, 2) + block, bf16),
             pltpu.VMEM((2, count - 1, 2, 128), f32),
             pltpu.VMEM((2, 2, 128), f32),
+            pltpu.VMEM((EARLY,) + block, f32),
             pltpu.SemaphoreType.DMA((4,)),
             pltpu.SemaphoreType.DMA((8,)),
             pltpu.SemaphoreType.DMA((12,)),
             pltpu.SemaphoreType.DMA((2,)),
             pltpu.SemaphoreType.DMA((2,)),
+            pltpu.SemaphoreType.DMA((EARLY,)),
+            pltpu.SemaphoreType.DMA((EARLY,)),
+            pltpu.SemaphoreType.REGULAR(((count - 1).bit_length(),)),
         ],
         compiler_params=pltpu.CompilerParams(
             collective_id=0, has_side_effects=True, vmem_limit_bytes=60 * 1024 * 1024

time: 51.6 us -> 48.2 us (0.934)
  Pallas kernels: 50.8 us -> 47.4 us
    pallas_call x1, Pallas kernels: 49.9 us -> 46.5 us  [on_device(): pl.pallas_call(kernel, out_shape=(pltpu.VMEM((2,) + block, f32), pltpu.VM...]
where the time goes in v3:
time: 48.2 us; the launch traced here: 48 us
  Pallas kernels  47.4 us (98%)
  between operations  0.64 us (1%)
    pallas_call x1, Pallas kernels, on_device(): pl.pallas_call(kernel, out_shape=(pltpu.VMEM((2,) + block, f32), pltpu.VM...  46.5 us

profile of v3, /device:TPU:0, one launch (start us, length us, event | category | flops | bytes accessed | tf_op | source)
XLA Modules:
  0.0 48.0 jit_solution(13873248974382583065)
XLA Ops:
  0.6 46.5 %bond_update.1 = (f32[2,256,256]{2,1,0:T(8,128)S(1)}, f32[256,256]{1,0:T(8,128)S(1)}) custom-call(s32[16]{0:T(128)} %size_hbm.1, f32[1,2,256,256]{3,2,1,0:T(8,128)} %site_hbm.1, f32[1,14,256,256]{3,2,1,0:T(8,128)} %left_hbm.1, f32[1,14,256,256]{3,2,1,0:T(8,128)} %right_hbm.1), custom_call_target="tpu_custom_call" | custom-call | tf_op jit(solution)/shard_map/bond_update/pallas_call | solution.py:574
  47.1 0.9 %write_out.1 = (f32[1,2,256,256]{3,2,1,0:T(8,128)}, f32[1,256,256]{2,1,0:T(8,128)}) custom-call(f32[2,256,256]{2,1,0:T(8,128)S(1)} %get-tuple-element.4.left, f32[256,256]{1,0:T(8,128)S(1)} %get-tuple-element.5.bond), custom_call_target="tpu_custom_call" | custom-call | tf_op jit(solution)/shard_map/write_out/pallas_call | solution.py:619

commit v4 on v3

--- a/solution.py
+++ b/solution.py
@@ -91,7 +91,7 @@
     left_out, bond_out,
     size_ref, site, gram_own, gram_in, left_f, right_f, left_s, right_s, aug, fac, bond_own, bond_in, inv_own, inv_in,
     bond, applied, applied_in, acc, field_s, red_in, red_own, relayed,
-    local_sem, send_sem, recv_sem, red_send, red_recv, relay_send, relay_recv, greetings,
+    local_sem, send_sem, recv_sem, red_send, red_recv, relay_send, relay_recv, greetings, go,
 ):
     count = lax.axis_size("row")
     me = lax.axis_index("row")
@@ -112,6 +112,16 @@
     for load in loads:
         load.start()
 
+    quads = count // QUAD
+    quad, place = me // QUAD, lax.rem(me, QUAD)
+    goes_up = quad * SIDE // quads if count % QUAD == 0 else 0 * quad
+    goes_down = SIDE - (quad + 1) * SIDE // quads if count % QUAD == 0 else 0 * quad
+    relays_up, relays_down = place == QUAD - 1, place == 0
+    paired = relays_up | relays_down if count % QUAD == 0 else me < 0
+    across = jnp.clip(jnp.where(relays_up, me - QUAD + 1, me + QUAD - 1), 0, count - 1)
+    frees = ((place == 1) & (me + QUAD - 1 < count), (place == 2) & (me >= QUAD - 1))
+    over = (jnp.minimum(me + QUAD - 1, count - 1), jnp.maximum(me - QUAD + 1, 0))
+
     barrier = pltpu.get_barrier_semaphore()
 
     def greet(semaphore, distance):
@@ -121,9 +131,9 @@
             def _():
                 pl.semaphore_signal(semaphore, inc=1, device_id={"row": peer}, device_id_type=MESH)
 
-    def greeted(semaphore, distance):
+    def greeted(semaphore, distance, more=0):
         peers_of = jnp.where(me >= distance, 1, 0) + jnp.where(me < count - distance, 1, 0)
-        pl.semaphore_wait(semaphore, peers_of)
+        pl.semaphore_wait(semaphore, peers_of + more)
 
     levels = (count - 1).bit_length()
 
@@ -133,6 +143,11 @@
             greet(greetings.at[level + 1], 2 ** (level + 1))
 
     greet(barrier, 1)
+
+    @pl.when(paired)
+    def _():
+        pl.semaphore_signal(barrier, inc=1, device_id={"row": across}, device_id_type=MESH)
+
 
     def remote(source, target, sent, received, peer):
         return pltpu.make_async_remote_copy(
@@ -165,14 +180,8 @@
     def applied_sent(side):
         return remote(applied, applied_in.at[side], 5 + side, 7 + 2 * side, to_right)
 
-    quads = count // QUAD
-    quad, place = me // QUAD, lax.rem(me, QUAD)
-    goes_up = quad * SIDE // quads if count % QUAD == 0 else 0 * quad
-    goes_down = SIDE - (quad + 1) * SIDE // quads if count % QUAD == 0 else 0 * quad
-    relays_up, relays_down = place == QUAD - 1, place == 0
     by_relay = (jnp.where(relays_up, goes_down, 0), jnp.where(relays_down, goes_up, 0))
     relay_amount = jnp.where(relays_up, goes_up, jnp.where(relays_down, goes_down, 0))
-    across = jnp.clip(jnp.where(relays_up, me - QUAD + 1, me + QUAD - 1), 0, count - 1)
     beyond = jnp.clip(jnp.where(relays_up, me - QUAD, me + QUAD), 0, count - 1)
     relay_side = jnp.where(relays_up, 1, 0)
 
@@ -190,12 +199,15 @@
             device_id={"row": beyond}, device_id_type=MESH,
         )
 
-    def start_early(side):
+    def start_relayed(side):
         for k in range(EARLY):
 
             @pl.when(k < by_relay[side])
             def _():
                 to_relay(side, k).start()
+
+    def start_early(side):
+        for k in range(EARLY):
 
             @pl.when(k >= by_relay[side])
             def _():
@@ -249,12 +261,19 @@
         gram_own, jnp.where(block_column >= block_row, gram[:half, :half], gram[half:, half:]),
         gram[:half, half:], diagonal_rows(gram[half:, half:]),
     )
-    greeted(barrier, 1)
+    greeted(barrier, 1, jnp.where(paired, 1, 0))
     greet(greetings.at[0], 1)
+    start_relayed(0)
+
+    waits_down, waits_up = not_last & (place == 1), not_first & (place == 2)
 
     @pl.when(not_last)
     def _():
         send_gram.start()
+
+    @pl.when(not_last & ~waits_down)
+    def _():
+        start_early(0)
 
     upper = jnp.where(live_pair, site[0], 0.0)
     site[0] = upper
@@ -262,29 +281,19 @@
     gram = gram + jnp.where((row == column) & (row >= size), 1.0, 0.0)
     aug[:, states:] = jnp.where(row == column, 1.0, 0.0).astype(f32)
     fac[...] = jnp.zeros_like(fac)
+    start_relayed(1)
+
+    @pl.when(not_first & ~waits_up)
+    def _():
+        start_early(1)
+
     know(0)
 
-    @pl.when(not_last)
-    def _():
-        send_gram.wait_send()
+    @pl.when(not_first)
+    def _():
+        send_gram.wait_recv()
 
     know(1)
-
-    waits_down, waits_up = not_last & (place == 1), not_first & (place == 2)
-
-    @pl.when(not_last & ~waits_down)
-    def _():
-        start_early(0)
-
-
-    @pl.when(not_first)
-    def _():
-        send_gram.wait_recv()
-
-    @pl.when(not_first & ~waits_up)
-    def _():
-        start_early(1)
-
     block = gram_in[:half, :half]
     mirrored = block.T
     top_left = jnp.where(block_column >= block_row, block, mirrored)
@@ -311,17 +320,18 @@
         store_split(right_s, mine, right_f[mine])
         return carry
 
-    lax.fori_loop(0, panels, first_half, 0)
+    lax.fori_loop(0, panels // 2, first_half, 0)
+
+    @pl.when(waits_down)
+    def _():
+        start_early(0)
+
+    @pl.when(waits_up)
+    def _():
+        start_early(1)
+
+    lax.fori_loop(panels // 2, panels, first_half, 0)
     know(2)
-
-    @pl.when(waits_down)
-    def _():
-        start_early(0)
-
-    @pl.when(waits_up)
-    def _():
-        start_early(1)
-
     lax.fori_loop(panels, 2 * panels, second_half, 0)
     for level in range(3, levels):
         know(level)
@@ -418,6 +428,14 @@
         for k in range(EARLY):
             total = add_terms(total, 1 + side, side * SIDE + k)
         acc[...] = total
+        if order == 1:
+            for s in range(2):
+
+                @pl.when(frees[s])
+                def _():
+                    blocks_sent(s).wait_send()
+                    pl.semaphore_signal(go, inc=1, device_id={"row": over[s]}, device_id_type=MESH)
+
 
         @pl.when(there)
         def _():
@@ -468,6 +486,14 @@
     first_own = (channels - moved) // 2
     add_range(0, moved, first_own)
     add_range(0, moved + first_own, channels - moved - first_own)
+    for s in range(2):
+
+        @pl.when(held[s])
+        def _():
+            pl.semaphore_wait(go, 1)
+            for one in send_applied[s]:
+                one.start()
+
 
     for order, (side, there) in enumerate(sides):
         for part, rows in enumerate(halves):
@@ -475,14 +501,6 @@
             @pl.when(there)
             def _():
                 applied_copy(side, part, to_right).wait_recv()
-
-            if order == 0 and part == 0:
-                for s in range(2):
-
-                    @pl.when(held[s])
-                    def _():
-                        for one in send_applied[s]:
-                            one.start()
 
             if order == 1 and part == 1:
 
@@ -532,13 +550,19 @@
 
     @pl.when(not_last)
     def _():
-        for one in [blocks_sent(0), send_bond[0], applied_sent(0)]:
+        for one in [send_gram, send_bond[0], applied_sent(0)]:
             one.wait_send()
 
     @pl.when(not_first)
     def _():
-        for one in [blocks_sent(1), send_bond[1], applied_sent(1), send_inv]:
+        for one in [send_bond[1], applied_sent(1), send_inv]:
             one.wait_send()
+
+    for s, there in enumerate((not_last, not_first)):
+
+        @pl.when(there & ~frees[s])
+        def _():
+            blocks_sent(s).wait_send()
 
     for k in range(EARLY):
 
@@ -610,6 +634,7 @@
             pltpu.SemaphoreType.DMA((EARLY,)),
             pltpu.SemaphoreType.DMA((EARLY,)),
             pltpu.SemaphoreType.REGULAR(((count - 1).bit_length(),)),
+            pltpu.SemaphoreType.REGULAR,
         ],
         compiler_params=pltpu.CompilerParams(
             collective_id=0, has_side_effects=True, vmem_limit_bytes=60 * 1024 * 1024

time: 48.2 us -> 45.4 us (0.942)
  Pallas kernels: 47.4 us -> 44.6 us
    pallas_call x1, Pallas kernels: 46.5 us -> 43.7 us  [on_device(): pl.pallas_call(kernel, out_shape=(pltpu.VMEM((2,) + block, f32), pltpu.VM...]
where the time goes in v4:
time: 45.4 us; the launch traced here: 45.2 us
  Pallas kernels  44.6 us (98%)
  between operations  0.64 us (1%)
    pallas_call x1, Pallas kernels, on_device(): pl.pallas_call(kernel, out_shape=(pltpu.VMEM((2,) + block, f32), pltpu.VM...  43.7 us

profile of v4, /device:TPU:0, one launch (start us, length us, event | category | flops | bytes accessed | tf_op | source)
XLA Modules:
  0.0 45.2 jit_solution(15717126502307885988)
XLA Ops:
  0.6 43.7 %bond_update.1 = (f32[2,256,256]{2,1,0:T(8,128)S(1)}, f32[256,256]{1,0:T(8,128)S(1)}) custom-call(s32[16]{0:T(128)} %size_hbm.1, f32[1,2,256,256]{3,2,1,0:T(8,128)} %site_hbm.1, f32[1,14,256,256]{3,2,1,0:T(8,128)} %left_hbm.1, f32[1,14,256,256]{3,2,1,0:T(8,128)} %right_hbm.1), custom_call_target="tpu_custom_call" | custom-call | tf_op jit(solution)/shard_map/bond_update/pallas_call | solution.py:598
  44.4 0.9 %write_out.1 = (f32[1,2,256,256]{3,2,1,0:T(8,128)}, f32[1,256,256]{2,1,0:T(8,128)}) custom-call(f32[2,256,256]{2,1,0:T(8,128)S(1)} %get-tuple-element.4.left, f32[256,256]{1,0:T(8,128)S(1)} %get-tuple-element.5.bond), custom_call_target="tpu_custom_call" | custom-call | tf_op jit(solution)/shard_map/write_out/pallas_call | solution.py:644

commit v5 on v4

--- a/solution.py
+++ b/solution.py
@@ -90,7 +90,7 @@
     size_hbm, site_hbm, left_hbm, right_hbm,
     left_out, bond_out,
     size_ref, site, gram_own, gram_in, left_f, right_f, left_s, right_s, aug, fac, bond_own, bond_in, inv_own, inv_in,
-    bond, applied, applied_in, acc, field_s, red_in, red_own, relayed,
+    bond, applied, applied_in, acc, field_s, red_in, red_own, relayed, prepared,
     local_sem, send_sem, recv_sem, red_send, red_recv, relay_send, relay_recv, greetings, go,
 ):
     count = lax.axis_size("row")
@@ -114,8 +114,10 @@
 
     quads = count // QUAD
     quad, place = me // QUAD, lax.rem(me, QUAD)
-    goes_up = quad * SIDE // quads if count % QUAD == 0 else 0 * quad
-    goes_down = SIDE - (quad + 1) * SIDE // quads if count % QUAD == 0 else 0 * quad
+    goes_up, goes_down = 0 * quad, 0 * quad
+    if count % QUAD == 0:
+        goes_up = jnp.minimum(quad * SIDE // quads, EARLY)
+        goes_down = jnp.minimum(SIDE - (quad + 1) * SIDE // quads, EARLY)
     relays_up, relays_down = place == QUAD - 1, place == 0
     paired = relays_up | relays_down if count % QUAD == 0 else me < 0
     across = jnp.clip(jnp.where(relays_up, me - QUAD + 1, me + QUAD - 1), 0, count - 1)
@@ -160,11 +162,15 @@
 
     def block_copy(side, k, peer):
         a = side * SIDE + k
-        return remote(right_hbm.at[0, a], right_f.at[a], 1 + side, (1 if k < EARLY else 3) + side, peer)
-
-    def blocks_sent(side):
-        channels_of = pl.ds(side * SIDE, SIDE)
-        return remote(right_hbm.at[0, channels_of], right_f.at[channels_of], 1 + side, 1 + side, to_right)
+        return remote(right_hbm.at[0, a], right_f.at[a], 1 + side, 1 + side, peer)
+
+    def late_copy(side, part, peer):
+        a, rows = side * SIDE + EARLY, halves[part]
+        return remote(right_hbm.at[0, a, rows], right_f.at[a, rows], 8 + 2 * side + part, 3 + side, peer)
+
+    def late_block(side):
+        a = side * SIDE + EARLY
+        return remote(right_hbm.at[0, a], right_f.at[a], 8 + 2 * side, 3 + side, to_right)
 
     def early_blocks(side):
         channels_of = pl.ds(side * SIDE, EARLY)
@@ -215,7 +221,8 @@
 
     send_gram = remote(gram_own, gram_in, 0, 0, to_right)
     send_inv = remote(inv_own, inv_in, 7, 11, to_left)
-    sends = [[block_copy(s, k, peers[s]) for k in range(SIDE)] for s in range(2)]
+    sends = [[block_copy(s, k, peers[s]) for k in range(EARLY)] for s in range(2)]
+    send_late = [[late_copy(s, part, peers[s]) for part in range(2)] for s in range(2)]
     send_bond = [bond_copy(s, peers[s]) for s in range(2)]
     send_applied = [[applied_copy(s, part, peers[s]) for part in range(2)] for s in range(2)]
 
@@ -344,12 +351,12 @@
 
     @pl.when(not_last)
     def _():
-        for one in [send_bond[0]] + sends[0][EARLY:]:
+        for one in [send_bond[0]] + send_late[0]:
             one.start()
 
     @pl.when(not_first)
     def _():
-        for one in [send_bond[1]] + sends[1][EARLY:]:
+        for one in [send_bond[1]] + send_late[1]:
             one.start()
 
     bond[...] = jnp.where(live_pair & (column >= row), fac[:, :states], 0.0)
@@ -406,6 +413,15 @@
     inv_own[:, half:] = inverse[half:, :half]
 
     for order, (side, there) in enumerate(sides):
+        if order == 1:
+            for s in range(2):
+
+                @pl.when(frees[s])
+                def _():
+                    early_blocks(s).wait_send()
+                    send_late[s][0].wait_send()
+                    pl.semaphore_signal(go, inc=1, device_id={"row": over[s]}, device_id_type=MESH)
+
 
         @pl.when(there)
         def _():
@@ -428,18 +444,10 @@
         for k in range(EARLY):
             total = add_terms(total, 1 + side, side * SIDE + k)
         acc[...] = total
-        if order == 1:
-            for s in range(2):
-
-                @pl.when(frees[s])
-                def _():
-                    blocks_sent(s).wait_send()
-                    pl.semaphore_signal(go, inc=1, device_id={"row": over[s]}, device_id_type=MESH)
-
 
         @pl.when(there)
         def _():
-            block_copy(side, EARLY, to_right).wait_recv()
+            late_block(side).wait_recv()
 
         last = side * SIDE + EARLY
         store_split(right_s, last, right_f[last])
@@ -481,11 +489,10 @@
         def _():
             send_applied[1][part].start()
 
-    acc[...] = jnp.zeros_like(acc)
-    put_field(0, applied[...])
-    first_own = (channels - moved) // 2
-    add_range(0, moved, first_own)
-    add_range(0, moved + first_own, channels - moved - first_own)
+    @pl.when(not_first & ~held[1])
+    def _():
+        send_inv.start()
+
     for s in range(2):
 
         @pl.when(held[s])
@@ -494,19 +501,29 @@
             for one in send_applied[s]:
                 one.start()
 
+    acc[...] = jnp.zeros_like(acc)
+    put_field(0, applied[...])
+    add_range(0, moved, channels - moved)
+
+    def collect(t):
+        all_reductions(t).wait_recv()
+        return jnp.sum(red_own[t] + jnp.sum(red_in[t], axis=0), axis=1, keepdims=True)
+
+    def prepare():
+        total = collect(0)
+        start_norm, energy = total[:1], total[1:] / total[:1]
+        shifted = applied[...] - energy * bond[...]
+        prepared[...] = bond[...] + TAU * shifted - (0.5 * TAU * TAU) * energy * (applied[...] + shifted)
+        return start_norm
 
     for order, (side, there) in enumerate(sides):
         for part, rows in enumerate(halves):
+            if order == 1 and part == 1:
+                start_norm = prepare()
 
             @pl.when(there)
             def _():
                 applied_copy(side, part, to_right).wait_recv()
-
-            if order == 1 and part == 1:
-
-                @pl.when(not_first)
-                def _():
-                    send_inv.start()
 
             which = 1 + side
             field_s[which, 0, rows], field_s[which, 1, rows] = split_2(applied_in[side, rows])
@@ -519,20 +536,15 @@
                 total = outside(total, l_high, l_low, m_high, m_low)
             acc[...] = total
 
-    def collect(t):
-        all_reductions(t).wait_recv()
-        return jnp.sum(red_own[t] + jnp.sum(red_in[t], axis=0), axis=1, keepdims=True)
-
-    total = collect(0)
-    start_norm = total[:1]
-    energy = total[1:] / start_norm
-    shifted = applied[...] - energy * bond[...]
-    second = jnp.where(live_pair, acc[...], 0.0) - energy * applied[...] - energy * shifted
-    acc[...] = bond[...] + TAU * shifted + (0.5 * TAU * TAU) * second
+    acc[...] = prepared[...] + (0.5 * TAU * TAU) * jnp.where(live_pair, acc[...], 0.0)
     red_own[1, :1] = row_sum(acc[...] * acc[...])
     red_own[1, 1:] = jnp.zeros((1, 128), f32)
     for one in reductions(1):
         one.start()
+
+    @pl.when(held[1])
+    def _():
+        send_inv.start()
 
 
     @pl.when(not_last)
@@ -560,9 +572,14 @@
 
     for s, there in enumerate((not_last, not_first)):
 
+        @pl.when(there)
+        def _():
+            send_late[s][1].wait_send()
+
         @pl.when(there & ~frees[s])
         def _():
-            blocks_sent(s).wait_send()
+            early_blocks(s).wait_send()
+            send_late[s][0].wait_send()
 
     for k in range(EARLY):
 
@@ -626,8 +643,9 @@
             pltpu.VMEM((2, count - 1, 2, 128), f32),
             pltpu.VMEM((2, 2, 128), f32),
             pltpu.VMEM((EARLY,) + block, f32),
+            pltpu.VMEM(block, f32),
             pltpu.SemaphoreType.DMA((4,)),
-            pltpu.SemaphoreType.DMA((8,)),
+            pltpu.SemaphoreType.DMA((12,)),
             pltpu.SemaphoreType.DMA((12,)),
             pltpu.SemaphoreType.DMA((2,)),
             pltpu.SemaphoreType.DMA((2,)),

time: 45.4 us -> 43.7 us (0.963)
  Pallas kernels: 44.6 us -> 42.9 us
    pallas_call x1, Pallas kernels: 43.7 us -> 42 us  [on_device(): pl.pallas_call(kernel, out_shape=(pltpu.VMEM((2,) + block, f32), pltpu.VM...]
where the time goes in v5:
time: 43.7 us; the launch traced here: 43.6 us
  Pallas kernels  42.9 us (98%)
  between operations  0.64 us (1%)
    pallas_call x1, Pallas kernels, on_device(): pl.pallas_call(kernel, out_shape=(pltpu.VMEM((2,) + block, f32), pltpu.VM...  42 us
    pallas_call x1, Pallas kernels, on_device(): pl.pallas_call(write_out, out_shape=(jax.ShapeDtypeStruct(site_tensor.sha...  0.89 us

profile of v5, /device:TPU:0, one launch (start us, length us, event | category | flops | bytes accessed | tf_op | source)
XLA Modules:
  0.0 43.6 jit_solution(1007170485897611635)
XLA Ops:
  0.6 42.0 %bond_update.1 = (f32[2,256,256]{2,1,0:T(8,128)S(1)}, f32[256,256]{1,0:T(8,128)S(1)}) custom-call(s32[16]{0:T(128)} %size_hbm.1, f32[1,2,256,256]{3,2,1,0:T(8,128)} %site_hbm.1, f32[1,14,256,256]{3,2,1,0:T(8,128)} %left_hbm.1, f32[1,14,256,256]{3,2,1,0:T(8,128)} %right_hbm.1), custom_call_target="tpu_custom_call" | custom-call | tf_op jit(solution)/shard_map/bond_update/pallas_call | solution.py:615
  42.7 0.9 %write_out.1 = (f32[1,2,256,256]{3,2,1,0:T(8,128)}, f32[1,256,256]{2,1,0:T(8,128)}) custom-call(f32[2,256,256]{2,1,0:T(8,128)S(1)} %get-tuple-element.4.left, f32[256,256]{1,0:T(8,128)S(1)} %get-tuple-element.5.bond), custom_call_target="tpu_custom_call" | custom-call | tf_op jit(solution)/shard_map/write_out/pallas_call | solution.py:662

commit v6 on v5

--- a/solution.py
+++ b/solution.py
@@ -90,7 +90,7 @@
     size_hbm, site_hbm, left_hbm, right_hbm,
     left_out, bond_out,
     size_ref, site, gram_own, gram_in, left_f, right_f, left_s, right_s, aug, fac, bond_own, bond_in, inv_own, inv_in,
-    bond, applied, applied_in, acc, field_s, red_in, red_own, relayed, prepared,
+    bond, applied, applied_in, acc, field_s, red_in, red_own, relayed, prepared, twice,
     local_sem, send_sem, recv_sem, red_send, red_recv, relay_send, relay_recv, greetings, go,
 ):
     count = lax.axis_size("row")
@@ -165,7 +165,7 @@
         return remote(right_hbm.at[0, a], right_f.at[a], 1 + side, 1 + side, peer)
 
     def late_copy(side, part, peer):
-        a, rows = side * SIDE + EARLY, halves[part]
+        a, rows = side * SIDE + EARLY, (slice(0, states // 4), slice(states // 4, states))[part]
         return remote(right_hbm.at[0, a, rows], right_f.at[a, rows], 8 + 2 * side + part, 3 + side, peer)
 
     def late_block(side):
@@ -386,25 +386,45 @@
         m_high, m_low = middle_of(which, a, slice(None))
         return outside(total, left_s[0, a], left_s[1, a], m_high, m_low)
 
-    def add_range(which, start, amount):
+    def add_range(target, which, start, amount):
         group = next(n for n in (3, 2, 1) if amount % n == 0)
 
         def some(g, carry):
-            total = acc[...]
+            total = target[...]
             for k in range(group):
                 total = add_terms(total, which, start + g * group + k)
-            acc[...] = total
+            target[...] = total
             return carry
 
         lax.fori_loop(0, amount // group, some, 0)
+
+    def side_half(side, there, part):
+        rows, which = halves[part], 1 + side
+
+        @pl.when(there)
+        def _():
+            applied_copy(side, part, to_right).wait_recv()
+
+        field_s[which, 0, rows], field_s[which, 1, rows] = split_2(applied_in[side, rows])
+        middles = [middle_of(which, side * SIDE + k, rows) for k in range(SIDE)]
+        total = twice[...]
+        for k in range(0, SIDE, 2):
+            pair = [side * SIDE + k, side * SIDE + k + 1]
+            l_high, l_low = (jnp.concatenate([left_s[i, a, :, rows] for a in pair], 1) for i in range(2))
+            m_high, m_low = (jnp.concatenate([middles[k + j][i] for j in range(2)], 0) for i in range(2))
+            total = outside(total, l_high, l_low, m_high, m_low)
+        twice[...] = total
+
+    near_first = place == 1 if count % QUAD == 0 else me < 0
 
     near = 1 - lax.rem(me, 2)
     has_side = [jnp.where(s == 0, not_first, not_last) for s in (near, 1 - near)]
     sides = list(zip((near, 1 - near), has_side))
 
     acc[...] = jnp.zeros_like(acc)
+    twice[...] = jnp.zeros_like(twice)
     put_field(0, bond[...])
-    add_range(0, moved, channels - moved)
+    add_range(acc, 0, moved, channels - moved)
     relay(2, EARLY)
     inverse = jnp.where(column <= row, fac[:, states:], 0.0)
     turned = ((1,), (1,))
@@ -444,6 +464,13 @@
         for k in range(EARLY):
             total = add_terms(total, 1 + side, side * SIDE + k)
         acc[...] = total
+        if order == 1:
+
+            @pl.when(near_first)
+            def _():
+                for part in range(2):
+                    side_half(near, has_side[0], part)
+
 
         @pl.when(there)
         def _():
@@ -501,9 +528,8 @@
             for one in send_applied[s]:
                 one.start()
 
-    acc[...] = jnp.zeros_like(acc)
     put_field(0, applied[...])
-    add_range(0, moved, channels - moved)
+    add_range(twice, 0, moved, channels - moved)
 
     def collect(t):
         all_reductions(t).wait_recv()
@@ -520,23 +546,16 @@
         for part, rows in enumerate(halves):
             if order == 1 and part == 1:
                 start_norm = prepare()
-
-            @pl.when(there)
-            def _():
-                applied_copy(side, part, to_right).wait_recv()
-
-            which = 1 + side
-            field_s[which, 0, rows], field_s[which, 1, rows] = split_2(applied_in[side, rows])
-            middles = [middle_of(which, side * SIDE + k, rows) for k in range(SIDE)]
-            total = acc[...]
-            for k in range(0, SIDE, 2):
-                pair = [side * SIDE + k, side * SIDE + k + 1]
-                l_high, l_low = (jnp.concatenate([left_s[i, a, :, rows] for a in pair], 1) for i in range(2))
-                m_high, m_low = (jnp.concatenate([middles[k + j][i] for j in range(2)], 0) for i in range(2))
-                total = outside(total, l_high, l_low, m_high, m_low)
-            acc[...] = total
-
-    acc[...] = prepared[...] + (0.5 * TAU * TAU) * jnp.where(live_pair, acc[...], 0.0)
+            if order == 0:
+
+                @pl.when(~near_first)
+                def _():
+                    side_half(side, there, part)
+
+            else:
+                side_half(side, there, part)
+
+    acc[...] = prepared[...] + (0.5 * TAU * TAU) * jnp.where(live_pair, twice[...], 0.0)
     red_own[1, :1] = row_sum(acc[...] * acc[...])
     red_own[1, 1:] = jnp.zeros((1, 128), f32)
     for one in reductions(1):
@@ -644,6 +663,7 @@
             pltpu.VMEM((2, 2, 128), f32),
             pltpu.VMEM((EARLY,) + block, f32),
             pltpu.VMEM(block, f32),
+            pltpu.VMEM(block, f32),
             pltpu.SemaphoreType.DMA((4,)),
             pltpu.SemaphoreType.DMA((12,)),
             pltpu.SemaphoreType.DMA((12,)),

time: 43.7 us -> 43.8 us (level)
  no operation moved by 1% of the time
where the time goes in v6:
time: 43.8 us; the launch traced here: 43.6 us
  Pallas kernels  43 us (98%)
  between operations  0.64 us (1%)
    pallas_call x1, Pallas kernels, on_device(): pl.pallas_call(kernel, out_shape=(pltpu.VMEM((2,) + block, f32), pltpu.VM...  42.1 us
    pallas_call x1, Pallas kernels, on_device(): pl.pallas_call(write_out, out_shape=(jax.ShapeDtypeStruct(site_tensor.sha...  0.89 us

profile of v6, /device:TPU:0, one launch (start us, length us, event | category | flops | bytes accessed | tf_op | source)
XLA Modules:
  0.0 43.6 jit_solution(15112591455584451501)
XLA Ops:
  0.6 42.1 %bond_update.1 = (f32[2,256,256]{2,1,0:T(8,128)S(1)}, f32[256,256]{1,0:T(8,128)S(1)}) custom-call(s32[16]{0:T(128)} %size_hbm.1, f32[1,2,256,256]{3,2,1,0:T(8,128)} %site_hbm.1, f32[1,14,256,256]{3,2,1,0:T(8,128)} %left_hbm.1, f32[1,14,256,256]{3,2,1,0:T(8,128)} %right_hbm.1), custom_call_target="tpu_custom_call" | custom-call | tf_op jit(solution)/shard_map/bond_update/pallas_call | solution.py:634
  42.7 0.9 %write_out.1 = (f32[1,2,256,256]{3,2,1,0:T(8,128)}, f32[1,256,256]{2,1,0:T(8,128)}) custom-call(f32[2,256,256]{2,1,0:T(8,128)S(1)} %get-tuple-element.4.left, f32[256,256]{1,0:T(8,128)S(1)} %get-tuple-element.5.bond), custom_call_target="tpu_custom_call" | custom-call | tf_op jit(solution)/shard_map/write_out/pallas_call | solution.py:682
